TPU v7x, 32 devices: a whole 2x2x4 slice. The times are simulated.
32 devices in a mesh: dp: 2 (over x), kvh: 4 (over z), seq: 4 (over y, core).
Axes of the slice: x: 2, y: 2, z: 4, core: 2. Of those that a mesh axis runs over, the one named last changes fastest.
Arguments:
- x_hidden: bfloat16 [256, 4096], P('dp'), parts along dimension 0
- seq_lens: int32 [256], P('dp'), parts along dimension 0
- k_cache: bfloat16 [256, 1024, 8, 128], P('dp', 'seq', 'kvh'), parts along dimension 0
- v_cache: bfloat16 [256, 1024, 8, 128], P('dp', 'seq', 'kvh'), parts along dimension 0
- w_q: bfloat16 [4096, 32, 128], P(None, ('kvh', 'seq'))
- w_o: bfloat16 [32, 128, 4096], P(('kvh', 'seq'))
Outputs:
- output: bfloat16 [256, 4096], P('dp'), parts along dimension 0
There are 2 independent parts. A program takes and returns all parts, laid end to end along the dimension named above; an argument that names none is the same for every part.
All inputs are finite; a program needn't handle non-finite values.
Results may differ from a plain program's by a relative error of at most 0.00365571.
Values are sent between devices in bfloat16 or wider.
A program may use at most 1 GiB of HBM per device.

v0:
```python
import jax
import jax.numpy as jnp
from jax import lax
from jax.sharding import PartitionSpec as P

ROPE_THETA = 500000.0
NEG_FILL = -1e30


def rotate_query(q_raw, seq_lens):
    half_dim = q_raw.shape[-1] // 2
    inv_freq = jnp.power(ROPE_THETA, -jnp.arange(half_dim, dtype=jnp.float32) * (2.0 / q_raw.shape[-1]))
    angle = (seq_lens - 1).astype(jnp.float32)[:, None] * inv_freq[None, :]
    cosine = jnp.cos(angle)[:, None, :]
    sine = jnp.sin(angle)[:, None, :]
    first = q_raw[..., :half_dim]
    second = q_raw[..., half_dim:]
    return jnp.concatenate([first * cosine - second * sine, second * cosine + first * sine], axis=-1)


def solution(mesh):
    def local_step(x_hidden, seq_lens, k_loc, v_loc, wq_loc, wo_loc):
        row_count = x_hidden.shape[0]
        t_dev = k_loc.shape[1]
        kv_loc = k_loc.shape[2]
        head_dim = k_loc.shape[3]
        q_raw = jnp.einsum('bd,dhk->bhk', x_hidden, wq_loc, preferred_element_type=jnp.float32)
        q_own = rotate_query(q_raw, seq_lens).astype(jnp.bfloat16)
        q_slice = lax.all_gather(q_own, 'seq', axis=1, tiled=True)
        slice_heads = q_slice.shape[1]
        q_grp = q_slice.reshape(row_count, kv_loc, slice_heads // kv_loc, head_dim)
        scores = jnp.einsum('bngk,btnk->bngt', q_grp, k_loc, preferred_element_type=jnp.float32) * (head_dim ** -0.5)
        positions = lax.axis_index('seq') * t_dev + jnp.arange(t_dev)
        valid_mask = (positions[None, :] < seq_lens[:, None])[:, None, None, :]
        scores = jnp.where(valid_mask, scores, NEG_FILL)
        local_max = jnp.max(scores, axis=-1)
        weights = jnp.where(valid_mask, jnp.exp(scores - local_max[..., None]), 0.0)
        local_sum = jnp.sum(weights, axis=-1)
        local_out = jnp.einsum('bngt,btnk->bngk', weights.astype(jnp.bfloat16), v_loc, preferred_element_type=jnp.float32)
        global_max = lax.pmax(local_max, 'seq')
        rescale = jnp.exp(local_max - global_max)
        out_part = (local_out * rescale[..., None]).reshape(row_count, slice_heads, head_dim)
        sum_part = (local_sum * rescale).reshape(row_count, slice_heads)
        out_own = lax.psum_scatter(out_part, 'seq', scatter_dimension=1, tiled=True)
        sum_own = lax.psum_scatter(sum_part, 'seq', scatter_dimension=1, tiled=True)
        attn = (out_own / sum_own[..., None]).astype(jnp.bfloat16)
        y_part = jnp.einsum('bhk,hkd->bd', attn, wo_loc, preferred_element_type=jnp.float32)
        y_sum = lax.psum(y_part, ('kvh', 'seq'))
        return (x_hidden.astype(jnp.float32) + y_sum).astype(jnp.bfloat16)

    return jax.shard_map(
        local_step,
        mesh=mesh,
        in_specs=(P('dp', None), P('dp'), P('dp', 'seq', 'kvh', None), P('dp', 'seq', 'kvh', None),
                  P(None, ('kvh', 'seq'), None), P(('kvh', 'seq'), None, None)),
        out_specs=P('dp', None),
        check_vma=False)
```

profile of v0, /device:TPU:0, one launch (start us, length us, event | category | flops | bytes accessed | tf_op | source)
XLA Modules:
  0.0 193.7 jit_solution(7872625863892627562)
XLA Ops:
  6.5 0.0 copy-start
  6.5 0.0 reduce-scatter.2.cloned.1.call-start
  6.6 0.8 add_convert_fusion.2
  7.4 1.3 broadcast_compare_fusion
  8.7 0.0 copy-start.1
  8.7 6.4 %copy.20 = bf16[4096,2,128]{0,2,1:T(8,128)(2,1)} copy(bf16[4096,2,128]{2,1,0:T(2,128)(2,1)} %param.10) | data formatting | bytes 4194304 | tf_op args[4]
  15.1 0.2 multiply_cosine_fusion
  15.3 0.0 copy-done.1
  15.3 2.3 %fusion.23 = f32[128,256]{0,1:S(1)} fusion(bf16[128,4096]{1,0:T(8,128)(2,1)S(1)} %copy-done.1, bf16[4096,256]{0,1:T(8,128)(2,1)} %bitcast.17), kind=kOutput, calls=%fused_computation.31 | convolution fusion | flops 268435456 | bytes 3276800
  17.6 0.1 copy.21
  17.8 7.3 %all_gather.3 = bf16[128,8,128]{2,0,1:T(8,128)(2,1)S(1)} all-gather(bf16[128,2,128]{2,0,1:T(8,128)(2,1)S(1)} %copy.21), channel_id=1, replica_groups=mesh['dp'=2,'kvh'=4,'seq'=4] {'seq'}, dimensions={1}, use_global_device_ids=true | all-gather | bytes 327680 | tf_op jit(solution)/shard_map/all_gather | solution.py:29
  25.0 0.2 copy.22
  25.2 11.3 %fusion.22 = (f32[128,2,4]{2,1,0:T(2,128)S(1)}, f32[128,2,4,256]{3,2,1,0:T(4,128)}) fusion(bf16[128,2,4,128]{3,2,1,0:T(4,128)(2,1)S(1)} %bitcast.24, bf16[128,256,2,128]{3,2,1,0:T(2,128)(2,1)} %param.8, pred[128,256]{1,0:T(8,128)(4,1)} %broadcast_compare_fusion), kind=kOutput, calls=%fused_computation.30 | convolution fusion | flops 67894272 | bytes 18124800 | tf_op jit(solution)/shard_map/bngk,btnk->bngt/dot_general | solution.py:32
  36.5 12.9 %pmax.7 = f32[128,2,4]{2,1,0:T(2,128)S(1)} all-reduce(f32[128,2,4]{2,1,0:T(2,128)S(1)} %get-tuple-element.11), channel_id=1, replica_groups=mesh['dp'=2,'kvh'=4,'seq'=4] {'seq'}, use_global_device_ids=true, to_apply=%region_1.2 | all-reduce | flops 1024 | bytes 8192 | tf_op jit(solution)/shard_map/pmax | solution.py:40
  49.4 2.0 %fusion.13 = f32[128,2,4]{2,1,0:T(2,128)S(1)} fusion(f32[128,2,4,256]{3,2,1,0:T(4,128)} %get-tuple-element.12, f32[128,2,4]{2,1,0:T(2,128)S(1)} %get-tuple-element.11, pred[128,256]{1,0:T(8,128)(4,1)} %broadcast_compare_fusion), kind=kLoop, calls=%fused_computation.10 | loop fusion | flops 785408 | bytes 1089536 | tf_op jit(solution)/shard_map/reduce_sum | solution.py:38
  51.5 0.0 copy-start.2
  51.5 8.5 %fusion.7 = f32[128,2,4,128]{3,2,1,0:T(4,128)S(1)} fusion(bf16[128,256,2,128]{3,2,1,0:T(2,128)(2,1)} %param.9, f32[128,2,4,256]{3,2,1,0:T(4,128)} %get-tuple-element.12, f32[128,2,4]{2,1,0:T(2,128)S(1)} %get-tuple-element.11, pred[128,256]{1,0:T(8,128)(4,1)} %broadcast_compare_fusion, f32[128,2,4]{2,1,0:T(2,128)S(1)} %bitcast.25), kind=kOutput, calls=%fused_computation.7 | convolution fusion | flops 68026368 | bytes 18391040 | tf_op jit(solution)/shard_map/bngt,btnk->bngk/dot_general | solution.py:39
  60.0 0.9 copy.25
  60.9 0.0 reduce-scatter.2.cloned.1.call-update
  60.9 0.0 all-reduce.3.cloned.1.call-start
  61.0 0.1 copy.26
  61.0 0.0 copy-done.2
  61.0 0.7 dynamic-slice
  62.4 6.0 %all-reduce = f32[128,8]{0,1:T(8,128)S(1)} all-reduce(f32[128,8]{0,1:T(8,128)S(1)} %bitcast.26), channel_id=3, replica_groups=mesh['dp'=2,'kvh'=4,'seq'=4] {'seq'}, use_global_device_ids=true, to_apply=%region_4.5.clone | all-reduce | flops 1024 | bytes 8192
  68.4 14.6 %reduce-scatter.2.cloned.1.call-done = f32[128,2,128]{2,0,1:T(8,128)} async-done(((f32[128,8,128]{2,0,1:T(8,128)}), f32[128,2,128]{2,0,1:T(8,128)}) %reduce-scatter.2.cloned.1.call-update) | async-done | bytes 131088 | tf_op jit(solution)/shard_map/reduce_scatter | solution.py:44
  83.0 0.0 copy-done
  83.0 2.8 %convolution_bitcast_fusion = f32[128,4096]{1,0:T(8,128)} fusion(bf16[2,128,4096]{2,1,0:T(8,128)(2,1)S(1)} %copy-done, f32[128,2,128]{2,0,1:T(8,128)} %reduce-scatter.2.cloned.1.call-done, f32[128,2]{0,1:T(2,128)S(1)} %constant_dynamic-slice_fusion), kind=kOutput, calls=%fused_computation.4 | convolution fusion | flops 268500992 | bytes 4326400 | tf_op jit(solution)/shard_map/bhk,hkd->bd/dot_general | solution.py:47
  85.7 0.0 all-reduce.3.cloned.1.call-update
  85.7 98.4 %all-reduce.3.cloned.1.call-done = f32[128,4096]{1,0:T(8,128)} async-done(((f32[128,4096]{1,0:T(8,128)}), f32[128,4096]{1,0:T(8,128)}) %all-reduce.3.cloned.1.call-update) | async-done | bytes 2097168 | tf_op jit(solution)/shard_map/psum | solution.py:48
  184.1 2.8 %add_convert_fusion = bf16[128,4096]{1,0:T(8,128)(2,1)} fusion(f32[128,4096]{1,0:T(8,128)} %all-reduce.3.cloned.1.call-done, bf16[128,4096]{1,0:T(8,128)(2,1)S(1)} %copy-done.1), kind=kLoop, calls=%fused_computation.5 | loop fusion | flops 1572864 | bytes 4194304 | tf_op jit(solution)/shard_map/convert_element_type | solution.py:49
  (6 shorter events, 0.1 us)
Async XLA Ops:
  6.5 76.4 %copy-start = (bf16[2,128,4096]{2,1,0:T(8,128)(2,1)S(1)}, bf16[2,128,4096]{2,1,0:T(8,128)(2,1)}, u32[]{:S(2)}) copy-start(bf16[2,128,4096]{2,1,0:T(8,128)(2,1)} %param.11) | copy-start | bytes 6291460
  6.5 76.4 %reduce-scatter.2.cloned.1.call-start = ((), (), s32[]{:S(2)}) async-start(), calls=%async_computation.1 | async-start | bytes 655360 | tf_op jit(solution)/shard_map/reduce_scatter | solution.py:44
  8.7 6.6 %copy-start.1 = (bf16[128,4096]{1,0:T(8,128)(2,1)S(1)}, bf16[128,4096]{1,0:T(8,128)(2,1)}, u32[]{:S(2)}) copy-start(bf16[128,4096]{1,0:T(8,128)(2,1)} %param.6) | copy-start | bytes 3145732
  51.5 9.6 %copy-start.2 = (u32[32]{0:T(128)S(1)}, u32[32]{0:T(128)}, u32[]{:S(2)}) copy-start(u32[32]{0:T(128)} %constant.27) | copy-start | bytes 388
  60.9 123.2 %all-reduce.3.cloned.1.call-start = ((), (), s32[]{:S(2)}) async-start(), calls=%async_computation.2 | async-start | bytes 4194304 | tf_op jit(solution)/shard_map/psum | solution.py:48
Sparse Core Ops, SparseCore 0:
  61.0 21.8 reduce-scatter.1
  86.5 97.5 all-reduce.2
where the time goes:
time: 194 us
  waiting for transfers between devices  113 us (58%)
  blocking collectives  26.2 us (14%)
  matrix products  24.8 us (13%)
  between operations  14.2 us (7%)
  local copies, waits for them, and re-layouts  8.33 us (4%)
  other arithmetic  7.18 us (4%)
    psum x1, waiting for transfers between devices, local_step(): y_sum = lax.psum(y_part, ('kvh', 'seq'))  98.4 us
    reduce_scatter x1, waiting for transfers between devices, local_step(): out_own = lax.psum_scatter(out_part, 'seq', scatter_dimension=1, tiled=True)  14.6 us
    pmax x1, blocking collectives, local_step(): global_max = lax.pmax(local_max, 'seq')  12.9 us
    dot_general x1, matrix products, local_step(): jnp.einsum('bngk,btnk->bngt', q_grp, k_loc, preferred_element_type=jnp.fl...  11.3 us
    dot_general x1, matrix products, local_step(): jnp.einsum('bngt,btnk->bngk', weights.astype(jnp.bfloat16), v_loc, prefer...  8.51 us
    all_gather x1, blocking collectives, local_step(): q_slice = lax.all_gather(q_own, 'seq', axis=1, tiled=True)  7.28 us
    unnamed x9, local copies, waits for them, and re-layouts  7.06 us
    unnamed x1, blocking collectives  5.98 us
  transfers between devices with their start and end apart: 2, of which 2 were waited for; matrix products, arithmetic and copies ran while one was open for 0% of the time, Pallas kernels for 0%

commit v1 on v0

v1 whole, which is shorter than its diff:
```python
import math

import jax
import jax.numpy as jnp
from jax import lax
from jax.experimental import pallas as pl
from jax.experimental.pallas import tpu as pltpu
from jax.sharding import PartitionSpec as P

ROPE_THETA = 500000.0
NEG = -1e30
FLOOR = -1e29
F32 = jnp.float32
BF16 = jnp.bfloat16
MESH = pl.DeviceIdType.MESH

ROWS = 128
RB = 16
NC = ROWS // RB
T = 256
D = 4096
HD = 128
NW = 8
WR = 2 * D // NW
QH = 2
OR_ = 2 * RB + 8

SK_B, SK_C, SK_D, SK_E, SK_F, SK_G, SK_H = 2, 3, 5, 8, 11, 13, 14


def kernel(lens_s, x_h, k_h, v_h, wq_h, wo_h, out_h,
           x_v, k_v, v_v, wq_v, wf_v, wo_v, len_v, q_all,
           o_send, o_recv, at_own, at_peer, y_keep, y_send, y_recv,
           z_buf, z_recv, out_v,
           s_x, s_wq, s_k, s_v, s_wo, s_out,
           wo_ss, wo_rs, q_ss, q_rs, o_ss, o_rs, a_ss, a_rs, y_ss, y_rs,
           z_ss, z_rs, ez_ss, ez_rs, ey_ss, ey_rs, ec_ss, ec_rs, ed_ss, ed_rs):
    dp = lax.axis_index("dp")
    z = lax.axis_index("kvh")
    s = lax.axis_index("seq")
    yy = s // 2
    cc = s % 2
    half_c = cc * 2048
    own_col = half_c + yy * 1024
    oth_col = half_c + (1 - yy) * 1024
    peer_half = (1 - cc) * 2048

    def seq_dev(d):
        return (dp, z, (s + d) % 4)

    def z_dev(d):
        return (dp, (z + d) % 4, s)

    core_dev = (dp, z, yy * 2 + (1 - cc))
    y_dev = (dp, z, (1 - yy) * 2 + cc)

    barrier = pltpu.get_barrier_semaphore()
    for d in (1, 2, 3):
        pl.semaphore_signal(barrier, inc=1, device_id=seq_dev(d), device_id_type=MESH)
        pl.semaphore_signal(barrier, inc=1, device_id=z_dev(d), device_id_type=MESH)

    x_cp = pltpu.make_async_copy(x_h, x_v, s_x)
    x_cp.start()

    def wq_cp(i):
        return pltpu.make_async_copy(wq_h.at[pl.ds(i * WR, WR)], wq_v.at[pl.ds(i * WR, WR)], s_wq.at[i])

    for i in range(NW):
        wq_cp(i).start()

    def k_cp(c):
        return pltpu.make_async_copy(k_h.at[pl.ds(c * RB, RB)], k_v.at[pl.ds(c * RB, RB)], s_k.at[c])

    def v_cp(c):
        return pltpu.make_async_copy(v_h.at[pl.ds(c * RB, RB)], v_v.at[pl.ds(c * RB, RB)], s_v.at[c])

    def wo_cp(i):
        col = pl.multiple_of(oth_col if i == 0 else own_col, 128)
        return pltpu.make_async_copy(wo_h.at[:, pl.ds(col, 1024)], wo_v.at[i, pl.ds(0, 256)], s_wo.at[i])

    def wo_rcp(i):
        col = pl.multiple_of(peer_half + ((1 - yy) if i == 0 else yy) * 1024, 128)
        return pltpu.make_async_remote_copy(
            wo_h.at[:, pl.ds(col, 1024)], wo_v.at[i, pl.ds(256, 256)],
            wo_ss.at[i], wo_rs.at[i], device_id=core_dev, device_id_type=MESH)

    for c in range(NC):
        k_cp(c).start()
        v_cp(c).start()
        if c == 2:
            for i in range(2):
                wo_cp(i).start()

    sub8 = lax.broadcasted_iota(jnp.int32, (8, 128), 0)
    lane8 = lax.broadcasted_iota(jnp.int32, (8, 128), 1)

    def len_body(g, carry):
        r0 = pl.multiple_of(g * 8, 8)
        acc = jnp.zeros((8, 128), jnp.int32)
        for b in range(8):
            acc = jnp.where(sub8 == b, lens_s[r0 + b], acc)
        len_v[pl.ds(r0, 8), :] = acc
        return carry

    lax.fori_loop(0, ROWS // 8, len_body, 0)

    lane = lax.broadcasted_iota(jnp.int32, (ROWS, HD), 1)
    inv_freq = jnp.exp((lane % 64).astype(F32) * (-math.log(ROPE_THETA) / 64.0))
    angle = (len_v[...] - 1).astype(F32) * inv_freq
    cosv = jnp.cos(angle)
    sinv = jnp.where(lane < 64, -jnp.sin(angle), jnp.sin(angle))

    x_cp.wait()
    q_raw = jnp.zeros((ROWS, 2 * HD), F32)
    for i in range(NW):
        wq_cp(i).wait()
        slot = i % 2
        wf_v[slot] = wq_v[pl.ds(i * WR, WR), :].astype(F32)
        w0 = wf_v[slot, pl.ds(0, WR // 2, 2), :].astype(BF16)
        w1 = wf_v[slot, pl.ds(1, WR // 2, 2), :].astype(BF16)
        w = jnp.concatenate([w0, w1], axis=1)
        q_raw = q_raw + jnp.dot(x_v[:, pl.ds(i * (WR // 2), WR // 2)], w, preferred_element_type=F32)
    for hh in range(2):
        qh = q_raw[:, hh * HD:(hh + 1) * HD]
        rot = pltpu.roll(qh, 64, 1)
        q_all[s, :, hh * HD:(hh + 1) * HD] = (qh * cosv + rot * sinv).astype(BF16)

    pl.semaphore_wait(barrier, 6)

    QR = ROWS // QH

    def q_cp(h, d, src):
        return pltpu.make_async_remote_copy(
            q_all.at[src, pl.ds(h * QR, QR)], q_all.at[src, pl.ds(h * QR, QR)],
            q_ss.at[h, d - 1], q_rs.at[h, d - 1], device_id=seq_dev(d), device_id_type=MESH)

    for h in range(QH):
        for d in (2, 1, 3):
            q_cp(h, d, s).start()
    for i in range(2):
        wo_rcp(i).start()

    scale = HD ** -0.5 * math.log2(math.e)
    col8 = lax.broadcasted_iota(jnp.int32, (8, 2 * T), 1)
    big = 1 << 20
    colkey = [jnp.where(col8 % 2 == n, col8 // 2, big) for n in range(2)]
    t_off = s * T
    row64 = lax.broadcasted_iota(jnp.int32, (64, HD), 0) % 8

    def o_cp(c, d):
        return pltpu.make_async_remote_copy(
            o_send.at[c, (s + d) % 4], o_recv.at[c, d - 1],
            o_ss.at[c, d - 1], o_rs.at[c, d - 1], device_id=seq_dev(d), device_id_type=MESH)

    def stage_a(c):
        for h in range(QH):
            @pl.when(c == h * (NC // QH))
            def _():
                for d in (1, 2, 3):
                    q_cp(h, d, (s + 4 - d) % 4).wait_recv()
        k_cp(c).wait()
        v_cp(c).wait()
        r0 = pl.multiple_of(c * RB, RB)
        qf = [q_all[i, pl.ds(r0, RB), :].astype(F32) for i in range(4)]
        scores = []
        for o in range(2):
            q64 = jnp.concatenate(
                [qf[i][8 * o:8 * o + 8, hh * HD:(hh + 1) * HD] for i in range(4) for hh in range(2)], axis=0)
            lhs = jnp.concatenate([jnp.where(row64 == b, q64, 0.0).astype(BF16) for b in range(8)], axis=1)
            kc = jnp.concatenate([k_v[r0 + 8 * o + b] for b in range(8)], axis=1)
            scores.append(lax.dot_general(lhs, kc, (((1,), (1,)), ((), ())), preferred_element_type=F32))
        probs = []
        ml = [jnp.zeros((8, 128), F32) for _ in range(4)]
        for o in range(2):
            lim = len_v[pl.ds(r0 + 8 * o, 8), :] - t_off
            lim = jnp.concatenate([lim] * 4, axis=1)
            mask = [colkey[n] < lim for n in range(2)]
            ps = []
            for g in range(8):
                zz = jnp.where(mask[g // 4], scores[o][8 * g:8 * g + 8, :] * scale, NEG)
                m = jnp.maximum(jnp.max(zz, axis=1, keepdims=True), FLOOR)
                p = jnp.exp2(zz - m)
                l = jnp.sum(p, axis=1, keepdims=True)
                ml[g // 2] = jnp.where(lane8 == 4 * o + g % 2, m, ml[g // 2])
                ml[g // 2] = jnp.where(lane8 == 4 * o + 2 + g % 2, l, ml[g // 2])
                ps.append(p)
            probs.append(jnp.concatenate(ps, axis=0).astype(BF16))
        for o in range(2):
            vc = jnp.concatenate([v_v[r0 + 8 * o + b] for b in range(8)], axis=1)
            res = jnp.dot(probs[o], vc, preferred_element_type=F32)
            acc = jnp.where(row64 == 0, res[:, :HD], 0.0)
            for b in range(1, 8):
                acc = jnp.where(row64 == b, res[:, b * HD:(b + 1) * HD], acc)
            for i in range(4):
                for hh in range(2):
                    g = 2 * i + hh
                    o_send[c, i, pl.ds(hh * RB + 8 * o, 8), :] = acc[8 * g:8 * g + 8]
        for i in range(4):
            o_send[c, i, pl.ds(2 * RB, 8), :] = ml[i]
        for d in (2, 3, 1):
            o_cp(c, d).start()

    def a_cp(c):
        rows = pl.ds(pl.multiple_of(c * RB, RB), RB)
        return pltpu.make_async_remote_copy(
            at_own.at[rows], at_peer.at[rows], a_ss.at[c], a_rs.at[c],
            device_id=core_dev, device_id_type=MESH)

    def stage_b(c):
        for d in (1, 2, 3):
            o_cp(c, d).wait_recv()
        mls = [o_send[c, s, pl.ds(2 * RB, 8), :]] + [o_recv[c, d, pl.ds(2 * RB, 8), :] for d in range(3)]
        mx = jnp.maximum(jnp.maximum(mls[0], mls[1]), jnp.maximum(mls[2], mls[3]))
        is_m = (lane8 % 4) < 2
        fs = [jnp.exp2(jnp.where(is_m, v - mx, 0.0)) for v in mls]
        tot = sum(f * pltpu.roll(v, 126, 1) for f, v in zip(fs, mls))
        tot = jnp.where(is_m, tot, 1.0)
        gs = [f / tot for f in fs]
        r0 = pl.multiple_of(c * RB, RB)
        for hh in range(2):
            parts = []
            for o in range(2):
                idx = 4 * o + hh
                rows = pl.ds(hh * RB + 8 * o, 8)
                acc = jnp.broadcast_to(gs[0][:, idx:idx + 1], (8, HD)) * o_send[c, s, rows, :]
                for d in range(3):
                    acc = acc + jnp.broadcast_to(gs[d + 1][:, idx:idx + 1], (8, HD)) * o_recv[c, d, rows, :]
                parts.append(acc)
            at_own[pl.ds(r0, RB), hh * HD:(hh + 1) * HD] = jnp.concatenate(parts, axis=0).astype(BF16)
        a_cp(c).start()

    def y_cp(c):
        return pltpu.make_async_remote_copy(
            y_send.at[c], y_recv.at[c], y_ss.at[c], y_rs.at[c], device_id=y_dev, device_id_type=MESH)

    def stage_c(c):
        @pl.when(c == 0)
        def _():
            for i in range(2):
                wo_cp(i).wait()
                wo_rcp(i).wait_recv()
        a_cp(c).wait_recv()
        r0 = pl.multiple_of(c * RB, RB)
        at = jnp.concatenate([at_own[pl.ds(r0, RB), :], at_peer[pl.ds(r0, RB), :]], axis=1)
        y_send[c] = jnp.dot(at, wo_v[0], preferred_element_type=F32)
        y_cp(c).start()
        y_keep[c] = jnp.dot(at, wo_v[1], preferred_element_type=F32)

    def z_cp(c, d):
        return pltpu.make_async_remote_copy(
            z_buf.at[c, (z + d) % 4], z_recv.at[c, d - 1],
            z_ss.at[c, d - 1], z_rs.at[c, d - 1], device_id=z_dev(d), device_id_type=MESH)

    def stage_d(c):
        y_cp(c).wait_recv()
        tot = y_keep[c] + y_recv[c]
        for i in range(4):
            z_buf[c, i] = tot[:, i * 256:(i + 1) * 256]
        for d in (2, 1, 3):
            z_cp(c, d).start()

    def ez_cp(c, d, src):
        rows = pl.ds(pl.multiple_of(c * RB, RB), RB)
        cols = pl.ds(pl.multiple_of(own_col + src * 256, 128), 256)
        return pltpu.make_async_remote_copy(
            out_v.at[rows, cols], out_v.at[rows, cols],
            ez_ss.at[c, d - 1], ez_rs.at[c, d - 1], device_id=z_dev(d), device_id_type=MESH)

    def stage_e(c):
        for d in (1, 2, 3):
            z_cp(c, d).wait_recv()
        r0 = pl.multiple_of(c * RB, RB)
        cols = pl.ds(pl.multiple_of(own_col + z * 256, 128), 256)
        tot = (z_buf[c, z] + z_recv[c, 0]) + (z_recv[c, 1] + z_recv[c, 2])
        out_v[pl.ds(r0, RB), cols] = (x_v[pl.ds(r0, RB), cols].astype(F32) + tot).astype(BF16)
        for d in (2, 1, 3):
            ez_cp(c, d, z).start()

    def quarter(c, col):
        return out_v.at[pl.ds(pl.multiple_of(c * RB, RB), RB), pl.ds(pl.multiple_of(col, 128), 1024)]

    def ey_cp(c, col):
        q = quarter(c, col)
        return pltpu.make_async_remote_copy(q, q, ey_ss.at[c], ey_rs.at[c], device_id=y_dev, device_id_type=MESH)

    def ec_cp(c, col):
        q = quarter(c, col)
        return pltpu.make_async_remote_copy(q, q, ec_ss.at[c], ec_rs.at[c], device_id=core_dev, device_id_type=MESH)

    def ed_cp(c, col):
        q = quarter(c, col)
        return pltpu.make_async_remote_copy(q, q, ed_ss.at[c], ed_rs.at[c], device_id=core_dev, device_id_type=MESH)

    def stage_f(c):
        for d in (1, 2, 3):
            ez_cp(c, d, (z + 4 - d) % 4).wait_recv()
        ey_cp(c, own_col).start()
        ec_cp(c, own_col).start()

    def stage_g(c):
        ey_cp(c, oth_col).wait_recv()
        ed_cp(c, oth_col).start()

    def out_cp(c):
        rows = pl.ds(pl.multiple_of(c * RB, RB), RB)
        return pltpu.make_async_copy(out_v.at[rows], out_h.at[rows], s_out.at[c])

    def stage_h(c):
        ec_cp(c, peer_half + yy * 1024).wait_recv()
        ed_cp(c, peer_half + (1 - yy) * 1024).wait_recv()
        out_cp(c).start()

    stages = ((0, stage_a), (SK_B, stage_b), (SK_C, stage_c), (SK_D, stage_d), (SK_E, stage_e),
              (SK_F, stage_f), (SK_G, stage_g), (SK_H, stage_h))

    def slot_body(k, carry):
        for skew, stage in stages:
            @pl.when(jnp.logical_and(k >= skew, k < NC + skew))
            def _():
                stage(k - skew)
        return carry

    lax.fori_loop(0, NC + SK_H, slot_body, 0)

    for h in range(QH):
        for d in (1, 2, 3):
            q_cp(h, d, s).wait_send()
    for i in range(2):
        wo_rcp(i).wait_send()

    def drain(c, carry):
        for d in (1, 2, 3):
            o_cp(c, d).wait_send()
            z_cp(c, d).wait_send()
            ez_cp(c, d, z).wait_send()
        a_cp(c).wait_send()
        y_cp(c).wait_send()
        ey_cp(c, own_col).wait_send()
        ec_cp(c, own_col).wait_send()
        ed_cp(c, oth_col).wait_send()
        out_cp(c).wait()
        return carry

    lax.fori_loop(0, NC, drain, 0)


def solution(mesh):
    def local_step(x_hidden, seq_lens, k_loc, v_loc, wq_loc, wo_loc):
        k2 = k_loc.reshape(ROWS, 2 * T, HD)
        v2 = v_loc.reshape(ROWS, 2 * T, HD)
        wq2 = wq_loc.reshape(2 * D, HD)
        wo2 = wo_loc.reshape(2 * HD, D)
        dma = pltpu.SemaphoreType.DMA
        any_spec = pl.BlockSpec(memory_space=pl.ANY)
        return pl.pallas_call(
            kernel,
            out_shape=jax.ShapeDtypeStruct((ROWS, D), BF16),
            in_specs=[pl.BlockSpec(memory_space=pltpu.SMEM)] + [any_spec] * 5,
            out_specs=any_spec,
            scratch_shapes=[
                pltpu.VMEM((ROWS, D), BF16),
                pltpu.VMEM((ROWS, 2 * T, HD), BF16),
                pltpu.VMEM((ROWS, 2 * T, HD), BF16),
                pltpu.VMEM((2 * D, HD), BF16),
                pltpu.VMEM((2, WR, HD), F32),
                pltpu.VMEM((2, 512, 1024), BF16),
                pltpu.VMEM((ROWS, 128), jnp.int32),
                pltpu.VMEM((4, ROWS, 2 * HD), BF16),
                pltpu.VMEM((NC, 4, OR_, HD), F32),
                pltpu.VMEM((NC, 3, OR_, HD), F32),
                pltpu.VMEM((ROWS, 2 * HD), BF16),
                pltpu.VMEM((ROWS, 2 * HD), BF16),
                pltpu.VMEM((NC, RB, 1024), F32),
                pltpu.VMEM((NC, RB, 1024), F32),
                pltpu.VMEM((NC, RB, 1024), F32),
                pltpu.VMEM((NC, 4, RB, 256), F32),
                pltpu.VMEM((NC, 3, RB, 256), F32),
                pltpu.VMEM((ROWS, D), BF16),
                dma(()), dma((NW,)), dma((NC,)), dma((NC,)), dma((2,)), dma((NC,)),
                dma((2,)), dma((2,)),
                dma((QH, 3)), dma((QH, 3)),
                dma((NC, 3)), dma((NC, 3)),
                dma((NC,)), dma((NC,)),
                dma((NC,)), dma((NC,)),
                dma((NC, 3)), dma((NC, 3)),
                dma((NC, 3)), dma((NC, 3)),
                dma((NC,)), dma((NC,)),
                dma((NC,)), dma((NC,)),
                dma((NC,)), dma((NC,)),
            ],
            compiler_params=pltpu.CompilerParams(
                collective_id=0, has_side_effects=True, vmem_limit_bytes=60 * 1024 * 1024),
            name="decode",
        )(seq_lens, x_hidden, k2, v2, wq2, wo2)

    return jax.shard_map(
        local_step,
        mesh=mesh,
        in_specs=(P('dp', None), P('dp'), P('dp', 'seq', 'kvh', None), P('dp', 'seq', 'kvh', None),
                  P(None, ('kvh', 'seq'), None), P(('kvh', 'seq'), None, None)),
        out_specs=P('dp', None),
        check_vma=False)
```

time: 194 us -> 61.6 us (0.32)
  waiting for transfers between devices: 113 us -> 0 us
  Pallas kernels: 0 us -> 58.6 us
  blocking collectives: 26.2 us -> 0 us
  matrix products: 24.8 us -> 0 us
  between operations: 14.2 us -> 0.01 us
  other arithmetic: 7.18 us -> 0 us
  local copies, waits for them, and re-layouts: 8.33 us -> 2.29 us
    psum x1 -> x0, waiting for transfers between devices: 98.4 us -> none  [local_step(): y_sum = lax.psum(y_part, ('kvh', 'seq'))]
    pallas_call x0 -> x1, Pallas kernels: none -> 58.6 us  [local_step(): pl.pallas_call(kernel, out_shape=jax.ShapeDtypeStruct((ROWS, D), BF16), i...]
    dot_general x3 -> x0, matrix products: 22.5 us -> none  [the longest x1 11.3 us: local_step(): jnp.einsum('bngk,btnk->bngt', q_grp, k_loc, preferred_element_type=jnp.fl...]
    reduce_scatter x1 -> x0, waiting for transfers between devices: 14.6 us -> none  [local_step(): out_own = lax.psum_scatter(out_part, 'seq', scatter_dimension=1, tiled=True)]
    pmax x1 -> x0, blocking collectives: 12.9 us -> none  [local_step(): global_max = lax.pmax(local_max, 'seq')]
    all_gather x1 -> x0, blocking collectives: 7.28 us -> none  [local_step(): q_slice = lax.all_gather(q_own, 'seq', axis=1, tiled=True)]
    unnamed x1 -> x0, blocking collectives: 5.98 us -> none
    unnamed x9 -> x1, local copies, waits for them, and re-layouts: 7.06 us -> 2.29 us
  transfers between devices with their start and end apart: 2 -> 0, of which waited for: 2 -> 0; matrix products, arithmetic and copies ran while one was open for 0% -> 0% of each run, Pallas kernels for 0% -> 0%
where the time goes in v1:
time: 61.6 us; the launch traced here: 60.9 us
  Pallas kernels  58.6 us (95%)
  local copies, waits for them, and re-layouts  2.29 us (4%)
    pallas_call x1, Pallas kernels, local_step(): pl.pallas_call(kernel, out_shape=jax.ShapeDtypeStruct((ROWS, D), BF16), i...  58.6 us
    unnamed x1, local copies, waits for them, and re-layouts  2.29 us

profile of v1, /device:TPU:0, one launch (start us, length us, event | category | flops | bytes accessed | tf_op | source)
XLA Modules:
  0.0 60.9 jit_solution(9848828900268764727)
XLA Ops:
  0.0 58.6 %decode.1 = bf16[128,4096]{1,0:T(8,128)(2,1)} custom-call(s32[128]{0:T(128)} %lens_s.1, bf16[128,4096]{1,0:T(8,128)(2,1)} %x_h.1, bf16[128,512,128]{2,1,0:T(8,128)(2,1)} %bitcast.4, bf16[128,512,128]{2,1,0:T(8,128)(2,1)} %bitcast.5, bf16[8192,128]{1,0:T(8,128)(2,1)} %bitcast.6, bf16[256,4096]{1,0:T(8,128)(2,1)} %bitcast.7), custom_call_target="tpu_custom_call" | custom-call | tf_op jit(solution)/shard_map/decode/pallas_call | solution.py:355
  58.6 2.3 %copy.8 = bf16[128,4096]{1,0:T(8,128)(2,1)} copy(bf16[128,4096]{1,0:T(8,128)(2,1)} %decode.1) | data formatting | bytes 2097152

commit v2 on v1

v2 whole, which is shorter than its diff:
```python
import math

import jax
import jax.numpy as jnp
from jax import lax
from jax.experimental import pallas as pl
from jax.experimental.pallas import tpu as pltpu
from jax.sharding import PartitionSpec as P

ROPE_THETA = 500000.0
NEG = -1e30
FLOOR = -1e29
F32 = jnp.float32
BF16 = jnp.bfloat16
MESH = pl.DeviceIdType.MESH

ROWS = 128
RB = 16
NC = ROWS // RB
T = 256
D = 4096
HD = 128
NW = 4
WR = 2 * D // NW
QH = NC
NX = 3
OR_ = 2 * RB + 8

Z_FIRST = (0, 1, 2)
NF = len(Z_FIRST)

WORK = (0.97, 0.17, 0.42, 0.1, 0.08, 0.03, 0.02, 0.01)
LAT = (2.4, 1.1, 2.4, 3.6, 3.4, 2.4, 1.1)
WIRE = (0.86, 0.1, 1.4, 1.4, 0.7, 0.7, 0.1)
LINK = (0, 1, 0, 2, 2, 0, 1)
Z_PATH = {2: (3.6, 2.8, 2), 3: (2.4, 0.35, 0)}
PRIO = (7, 6, 5, 4, 3, 2, 1, 0)
Q_AT, Q_STEP, KV_AT, KV_STEP = 6.0, 0.35, 3.5, 1.27


def event_order():
    ready = {(0, 0): max(Q_AT, KV_AT + KV_STEP)}
    link_free = [0.0, 0.0, 0.0]
    now, order, last = 0.0, [], len(WORK) - 1
    while ready:
        can = [e for e, t in ready.items() if t <= now]
        if not can:
            now = min(ready.values())
            continue
        stage, c = min(can, key=lambda e: (PRIO[e[0]], e[1]))
        del ready[stage, c]
        order.append((stage, c))
        now += WORK[stage] * (0.55 if stage == 0 and c in (0, NC) else 1.0)
        if stage == 0:
            if c < NC:
                n = min(c + 1, NC - 1)
                ready[0, c + 1] = max(Q_AT + Q_STEP * n, KV_AT + KV_STEP * (n + 1))
            if c == 0:
                continue
            c -= 1
        if stage < last:
            lat, wire, link = LAT[stage], WIRE[stage], LINK[stage]
            if c in Z_FIRST and stage in Z_PATH:
                lat, wire, link = Z_PATH[stage]
            start = max(now, link_free[link])
            link_free[link] = start + wire
            ready[stage + 1, c] = start + wire + lat
    return order


def kernel(lens_h, x_h, k_h, v_h, wq_h, wo_h, out_v,
           lens_s, x_v, k_v, v_v, wq_v, wf_v, wo_v, len_v, q_all,
           o_send, o_recv, at_own, at_peer, y_keep, y_send, y_recv,
           z_buf, z_recv, f_buf, f_recv, g_buf, g_recv, s_scr, p_scr,
           s_len, s_x, s_wq, s_k, s_v, s_wo,
           wo_ss, wo_rs, q_ss, q_rs, o_ss, o_rs, a_ss, a_rs, y_ss, y_rs,
           z_ss, z_rs, f_ss, g_ss, ez_ss, ez_rs, ey_ss, ey_rs, ec_ss, ec_rs, ed_ss, ed_rs):
    dp = lax.axis_index("dp")
    z = lax.axis_index("kvh")
    s = lax.axis_index("seq")
    yy = s // 2
    cc = s % 2
    half_c = cc * 2048
    own_col = half_c + yy * 1024
    oth_col = half_c + (1 - yy) * 1024
    peer_half = (1 - cc) * 2048

    def seq_dev(d):
        return (dp, z, (s + d) % 4)

    def z_dev(d):
        return (dp, (z + d) % 4, s)

    def arrived(ref, sem):
        pltpu.make_async_remote_copy(ref, ref, sem, sem, device_id=seq_dev(1), device_id_type=MESH).wait_recv()

    def sent(ref, sem):
        pltpu.make_async_remote_copy(ref, ref, sem, sem, device_id=seq_dev(1), device_id_type=MESH).wait_send()

    core_dev = (dp, z, yy * 2 + (1 - cc))
    y_dev = (dp, z, (1 - yy) * 2 + cc)

    def x_cp(i):
        cols = pl.ds(i * (WR // 2), WR // 2)
        return pltpu.make_async_copy(x_h.at[:, cols], x_v.at[:, cols], s_x.at[i])

    lens_cp = pltpu.make_async_copy(lens_h, lens_s, s_len)
    lens_cp.start()

    def wq_cp(i):
        return pltpu.make_async_copy(wq_h.at[pl.ds(i * WR, WR)], wq_v.at[pl.ds(i * WR, WR)], s_wq.at[i])

    def load_q(i, carry):
        cols = pl.ds(pl.multiple_of(i * (WR // 2), WR // 2), WR // 2)
        rows = pl.ds(pl.multiple_of(i * WR, WR), WR)
        pltpu.make_async_copy(x_h.at[:, cols], x_v.at[:, cols], s_x.at[i]).start()
        pltpu.make_async_copy(wq_h.at[rows], wq_v.at[rows], s_wq.at[i]).start()
        return carry

    lax.fori_loop(0, NW, load_q, 0)

    def k_cp(c):
        return pltpu.make_async_copy(k_h.at[pl.ds(c * RB, RB)], k_v.at[pl.ds(c * RB, RB)], s_k.at[c])

    def v_cp(c):
        return pltpu.make_async_copy(v_h.at[pl.ds(c * RB, RB)], v_v.at[pl.ds(c * RB, RB)], s_v.at[c])

    def wo_cp(i):
        col = pl.multiple_of(oth_col if i == 0 else own_col, 128)
        return pltpu.make_async_copy(wo_h.at[:, pl.ds(col, 1024)], wo_v.at[i, pl.ds(0, 256)], s_wo.at[i])

    def wo_rcp(i):
        col = pl.multiple_of(peer_half + ((1 - yy) if i == 0 else yy) * 1024, 128)
        return pltpu.make_async_remote_copy(
            wo_h.at[:, pl.ds(col, 1024)], wo_v.at[i, pl.ds(256, 256)],
            wo_ss, wo_rs, device_id=core_dev, device_id_type=MESH)

    barrier = pltpu.get_barrier_semaphore()
    for d in (1, 2, 3):
        pl.semaphore_signal(barrier, inc=1, device_id=seq_dev(d), device_id_type=MESH)
        pl.semaphore_signal(barrier, inc=1, device_id=z_dev(d), device_id_type=MESH)

    def load_body(c, carry):
        k_cp(c).start()
        v_cp(c).start()

        @pl.when(c == 2)
        def _():
            for i in range(2):
                wo_cp(i).start()
        return carry

    lax.fori_loop(0, NC, load_body, 0)
    lens_cp.wait()

    sub8 = lax.broadcasted_iota(jnp.int32, (8, 128), 0)
    lane8 = lax.broadcasted_iota(jnp.int32, (8, 128), 1)

    def len_body(g, carry):
        r0 = pl.multiple_of(g * 8, 8)
        acc = jnp.zeros((8, 128), jnp.int32)
        for b in range(8):
            acc = jnp.where(sub8 == b, lens_s[r0 + b], acc)
        len_v[pl.ds(r0, 8), :] = acc
        return carry

    lax.fori_loop(0, ROWS // 8, len_body, 0)

    lane = lax.broadcasted_iota(jnp.int32, (ROWS, HD), 1)
    inv_freq = jnp.exp((lane % 64).astype(F32) * (-math.log(ROPE_THETA) / 64.0))
    angle = (len_v[...] - 1).astype(F32) * inv_freq
    cosv = jnp.cos(angle)
    sinv = jnp.where(lane < 64, -jnp.sin(angle), jnp.sin(angle))

    q_raw = jnp.zeros((ROWS, 2 * HD), F32)
    for i in range(NW):
        x_cp(i).wait()
        wq_cp(i).wait()
        slot = i % 2
        wf_v[slot] = wq_v[pl.ds(i * WR, WR), :].astype(F32)
        w0 = wf_v[slot, pl.ds(0, WR // 2, 2), :].astype(BF16)
        w1 = wf_v[slot, pl.ds(1, WR // 2, 2), :].astype(BF16)
        w = jnp.concatenate([w0, w1], axis=1)
        q_raw = q_raw + jnp.dot(x_v[:, pl.ds(i * (WR // 2), WR // 2)], w, preferred_element_type=F32)
    for hh in range(2):
        qh = q_raw[:, hh * HD:(hh + 1) * HD]
        rot = pltpu.roll(qh, 64, 1)
        q_all[s, :, hh * HD:(hh + 1) * HD] = (qh * cosv + rot * sinv).astype(BF16)

    pl.semaphore_wait(barrier, 6)


    def q_cp(h, d, src):
        return pltpu.make_async_remote_copy(
            q_all.at[src, pl.ds(pl.multiple_of(h * RB, RB), RB)], q_all.at[src, pl.ds(pl.multiple_of(h * RB, RB), RB)],
            q_ss, q_rs.at[h], device_id=seq_dev(d), device_id_type=MESH)

    def send_q(h, carry):
        for d in (2, 1, 3):
            q_cp(h, d, s).start()
        return carry

    lax.fori_loop(0, QH, send_q, 0)
    for i in range(2):
        wo_rcp(i).start()

    scale = HD ** -0.5 * math.log2(math.e)
    col8 = lax.broadcasted_iota(jnp.int32, (8, 2 * T), 1)
    big = 1 << 20
    colkey = [jnp.where(col8 % 2 == n, col8 // 2, big) for n in range(2)]
    t_off = s * T
    row64 = lax.broadcasted_iota(jnp.int32, (64, HD), 0) % 8

    def o_cp(c, d):
        return pltpu.make_async_remote_copy(
            o_send.at[c, (s + d) % 4], o_recv.at[c, d - 1],
            o_ss, o_rs.at[c], device_id=seq_dev(d), device_id_type=MESH)

    def issue_scores(c):
        rows = pl.ds(c * RB, RB)
        arrived(q_all.at[pl.ds(0, 3), rows], q_rs.at[c])
        k_cp(c).wait()
        return pl.multiple_of(c * RB, RB)

    def scores(r0):
        qf = [q_all[i, pl.ds(r0, RB), :].astype(F32) for i in range(4)]
        for o in range(2):
            q64 = jnp.concatenate(
                [qf[i][8 * o:8 * o + 8, hh * HD:(hh + 1) * HD] for i in range(4) for hh in range(2)], axis=0)
            lhs = jnp.concatenate([jnp.where(row64 == b, q64, 0.0).astype(BF16) for b in range(8)], axis=1)
            kn = jnp.concatenate([k_v[r0 + 8 * o + b] for b in range(NX)], axis=1)
            res = lax.dot_general(lhs[:, :NX * HD], kn, (((1,), (1,)), ((), ())), preferred_element_type=F32)
            if NX < 8:
                kt = jnp.concatenate([k_v[r0 + 8 * o + b].T for b in range(NX, 8)], axis=0)
                res = res + jnp.dot(lhs[:, NX * HD:], kt, preferred_element_type=F32)
            s_scr[o] = res

    def softmax(c):
        r0 = pl.multiple_of(c * RB, RB)
        ml = [jnp.zeros((8, 128), F32) for _ in range(4)]
        for o in range(2):
            lim = len_v[pl.ds(r0 + 8 * o, 8), :] - t_off
            lim = jnp.concatenate([lim] * 4, axis=1)
            mask = [colkey[n] < lim for n in range(2)]
            for g2 in range(4):
                ps = []
                for g in (2 * g2, 2 * g2 + 1):
                    zz = jnp.where(mask[g // 4], s_scr[o, 8 * g:8 * g + 8, :] * scale, NEG)
                    m = jnp.maximum(jnp.max(zz, axis=1, keepdims=True), FLOOR)
                    p = jnp.exp2(zz - m)
                    l = jnp.sum(p, axis=1, keepdims=True)
                    ml[g // 2] = jnp.where(lane8 == 4 * o + g % 2, m, ml[g // 2])
                    ml[g // 2] = jnp.where(lane8 == 4 * o + 2 + g % 2, l, ml[g // 2])
                    ps.append(p)
                p_scr[o, 16 * g2:16 * g2 + 16, :] = jnp.concatenate(ps, axis=0).astype(BF16)
        for i in range(4):
            o_send[c, i, pl.ds(2 * RB, 8), :] = ml[i]

    def weighted(c):
        r0 = pl.multiple_of(c * RB, RB)
        for o in range(2):
            vc = jnp.concatenate([v_v[r0 + 8 * o + b] for b in range(8)], axis=1)
            res = jnp.dot(p_scr[o], vc, preferred_element_type=F32)
            acc = jnp.where(row64 == 0, res[:, :HD], 0.0)
            for b in range(1, 8):
                acc = jnp.where(row64 == b, res[:, b * HD:(b + 1) * HD], acc)
            for i in range(4):
                for hh in range(2):
                    g = 2 * i + hh
                    o_send[c, i, pl.ds(hh * RB + 8 * o, 8), :] = acc[8 * g:8 * g + 8]

    def send_o(c):
        for d in (2, 3, 1):
            o_cp(c, d).start()

    def attention(k):
        if k > 0:
            v_cp(k - 1).wait()
        if k < NC:
            r0 = issue_scores(k)
        if k > 0:
            softmax(k - 1)
        if k < NC:
            scores(r0)
        if k > 0:
            weighted(k - 1)
            send_o(k - 1)

    def a_cp(c):
        rows = pl.ds(pl.multiple_of(c * RB, RB), RB)
        return pltpu.make_async_remote_copy(
            at_own.at[rows], at_peer.at[rows], a_ss, a_rs.at[c],
            device_id=core_dev, device_id_type=MESH)

    def stage_b(c):
        arrived(o_recv.at[c], o_rs.at[c])
        mls = [o_send[c, s, pl.ds(2 * RB, 8), :]] + [o_recv[c, d, pl.ds(2 * RB, 8), :] for d in range(3)]
        mx = jnp.maximum(jnp.maximum(mls[0], mls[1]), jnp.maximum(mls[2], mls[3]))
        is_m = (lane8 % 4) < 2
        fs = [jnp.exp2(jnp.where(is_m, v - mx, 0.0)) for v in mls]
        tot = sum(f * pltpu.roll(v, 126, 1) for f, v in zip(fs, mls))
        tot = jnp.where(is_m, tot, 1.0)
        gs = [f / tot for f in fs]
        r0 = pl.multiple_of(c * RB, RB)
        for hh in range(2):
            parts = []
            for o in range(2):
                idx = 4 * o + hh
                rows = pl.ds(hh * RB + 8 * o, 8)
                acc = jnp.broadcast_to(gs[0][:, idx:idx + 1], (8, HD)) * o_send[c, s, rows, :]
                for d in range(3):
                    acc = acc + jnp.broadcast_to(gs[d + 1][:, idx:idx + 1], (8, HD)) * o_recv[c, d, rows, :]
                parts.append(acc)
            at_own[pl.ds(r0, RB), hh * HD:(hh + 1) * HD] = jnp.concatenate(parts, axis=0).astype(BF16)
        a_cp(c).start()

    def y_cp(c):
        return pltpu.make_async_remote_copy(
            y_send.at[c], y_recv.at[c], y_ss, y_rs.at[c], device_id=y_dev, device_id_type=MESH)

    def stage_c(c):
        if c == 0:
            for i in range(2):
                wo_cp(i).wait()
            arrived(wo_v.at[:, pl.ds(256, 256)], wo_rs)
        a_cp(c).wait_recv()
        r0 = pl.multiple_of(c * RB, RB)
        at = jnp.concatenate([at_own[pl.ds(r0, RB), :], at_peer[pl.ds(r0, RB), :]], axis=1)
        if c in Z_FIRST:
            for p in range(2):
                part = jnp.dot(at, wo_v[p], preferred_element_type=F32)
                for i in range(4):
                    f_buf[slot_f(c), i, p] = part[:, i * 256:(i + 1) * 256]
            for d in (2, 1, 3):
                f_cp(c, d).start()
            return
        y_send[c] = jnp.dot(at, wo_v[0], preferred_element_type=F32)
        y_cp(c).start()
        y_keep[c] = jnp.dot(at, wo_v[1], preferred_element_type=F32)

    def slot_f(c):
        return Z_FIRST.index(c)

    def f_cp(c, d):
        i = slot_f(c)
        return pltpu.make_async_remote_copy(
            f_buf.at[i, (z + d) % 4], f_recv.at[i, d - 1],
            f_ss, z_rs.at[c], device_id=z_dev(d), device_id_type=MESH)

    def g_cp(c):
        i = slot_f(c)
        return pltpu.make_async_remote_copy(
            g_buf.at[i, 0], g_recv.at[i], g_ss, y_rs.at[c], device_id=y_dev, device_id_type=MESH)

    def z_cp(c, d):
        return pltpu.make_async_remote_copy(
            z_buf.at[c, (z + d) % 4], z_recv.at[c, d - 1],
            z_ss, z_rs.at[c], device_id=z_dev(d), device_id_type=MESH)

    def stage_d(c):
        if c in Z_FIRST:
            i = slot_f(c)
            arrived(f_recv.at[i], z_rs.at[c])
            g_buf[i] = (f_buf[i, z] + f_recv[i, 0]) + (f_recv[i, 1] + f_recv[i, 2])
            g_cp(c).start()
            return
        y_cp(c).wait_recv()
        tot = y_keep[c] + y_recv[c]
        for i in range(4):
            z_buf[c, i] = tot[:, i * 256:(i + 1) * 256]
        for d in (2, 1, 3):
            z_cp(c, d).start()

    def ez_cp(c, d, src):
        rows = pl.ds(pl.multiple_of(c * RB, RB), RB)
        cols = pl.ds(pl.multiple_of(own_col + src * 256, 128), 256)
        return pltpu.make_async_remote_copy(
            out_v.at[rows, cols], out_v.at[rows, cols],
            ez_ss, ez_rs.at[c], device_id=z_dev(d), device_id_type=MESH)

    def stage_e(c):
        if c in Z_FIRST:
            arrived(g_recv.at[slot_f(c)], y_rs.at[c])
        else:
            arrived(z_recv.at[c], z_rs.at[c])
        r0 = pl.multiple_of(c * RB, RB)
        cols = pl.ds(pl.multiple_of(own_col + z * 256, 128), 256)
        if c in Z_FIRST:
            tot = g_buf[slot_f(c), 1] + g_recv[slot_f(c)]
        else:
            tot = (z_buf[c, z] + z_recv[c, 0]) + (z_recv[c, 1] + z_recv[c, 2])
        out_v[pl.ds(r0, RB), cols] = (x_v[pl.ds(r0, RB), cols].astype(F32) + tot).astype(BF16)
        for d in (2, 1, 3):
            ez_cp(c, d, z).start()

    def quarter(c, col):
        return out_v.at[pl.ds(pl.multiple_of(c * RB, RB), RB), pl.ds(pl.multiple_of(col, 128), 1024)]

    def ey_cp(c, col):
        q = quarter(c, col)
        return pltpu.make_async_remote_copy(q, q, ey_ss, ey_rs.at[c], device_id=y_dev, device_id_type=MESH)

    def ec_cp(c, col):
        q = quarter(c, col)
        return pltpu.make_async_remote_copy(q, q, ec_ss, ec_rs.at[c], device_id=core_dev, device_id_type=MESH)

    def ed_cp(c, col):
        q = quarter(c, col)
        return pltpu.make_async_remote_copy(q, q, ed_ss, ed_rs.at[c], device_id=core_dev, device_id_type=MESH)

    def stage_f(c):
        arrived(out_v.at[pl.ds(c * RB, RB), pl.ds(0, 768)], ez_rs.at[c])
        ey_cp(c, own_col).start()
        ec_cp(c, own_col).start()

    def stage_g(c):
        ey_cp(c, oth_col).wait_recv()
        ed_cp(c, oth_col).start()

    def stage_h(c):
        ec_cp(c, peer_half + yy * 1024).wait_recv()
        ed_cp(c, peer_half + (1 - yy) * 1024).wait_recv()

    stages = (attention, stage_b, stage_c, stage_d, stage_e, stage_f, stage_g, stage_h)
    for stage, c in event_order():
        stages[stage](c)

    sent(q_all.at[pl.ds(0, 3)], q_ss)
    sent(wo_v.at[:, pl.ds(0, 256)], wo_ss)
    sent(o_recv, o_ss)
    sent(at_own, a_ss)
    sent(y_send.at[pl.ds(0, NC - NF)], y_ss)
    sent(z_recv.at[pl.ds(0, NC - NF)], z_ss)
    sent(f_recv, f_ss)
    sent(g_recv, g_ss)
    sent(out_v.at[:, pl.ds(0, 768)], ez_ss)
    for sem in (ey_ss, ec_ss, ed_ss):
        sent(out_v.at[:, pl.ds(0, 1024)], sem)


def solution(mesh):
    def local_step(x_hidden, seq_lens, k_loc, v_loc, wq_loc, wo_loc):
        k2 = k_loc.reshape(ROWS, 2 * T, HD)
        v2 = v_loc.reshape(ROWS, 2 * T, HD)
        wq2 = wq_loc.reshape(2 * D, HD)
        wo2 = wo_loc.reshape(2 * HD, D)
        dma = pltpu.SemaphoreType.DMA
        any_spec = pl.BlockSpec(memory_space=pltpu.HBM)
        return pl.pallas_call(
            kernel,
            out_shape=jax.ShapeDtypeStruct((ROWS, D), BF16),
            in_specs=[any_spec] * 6,
            out_specs=pl.BlockSpec(memory_space=pltpu.VMEM),
            scratch_shapes=[
                pltpu.SMEM((ROWS,), jnp.int32),
                pltpu.VMEM((ROWS, D), BF16),
                pltpu.VMEM((ROWS, 2 * T, HD), BF16),
                pltpu.VMEM((ROWS, 2 * T, HD), BF16),
                pltpu.VMEM((2 * D, HD), BF16),
                pltpu.VMEM((2, WR, HD), F32),
                pltpu.VMEM((2, 512, 1024), BF16),
                pltpu.VMEM((ROWS, 128), jnp.int32),
                pltpu.VMEM((4, ROWS, 2 * HD), BF16),
                pltpu.VMEM((NC, 4, OR_, HD), F32),
                pltpu.VMEM((NC, 3, OR_, HD), F32),
                pltpu.VMEM((ROWS, 2 * HD), BF16),
                pltpu.VMEM((ROWS, 2 * HD), BF16),
                pltpu.VMEM((NC, RB, 1024), F32),
                pltpu.VMEM((NC, RB, 1024), F32),
                pltpu.VMEM((NC, RB, 1024), F32),
                pltpu.VMEM((NC, 4, RB, 256), F32),
                pltpu.VMEM((NC, 3, RB, 256), F32),
                pltpu.VMEM((NF, 4, 2, RB, 256), F32),
                pltpu.VMEM((NF, 3, 2, RB, 256), F32),
                pltpu.VMEM((NF, 2, RB, 256), F32),
                pltpu.VMEM((NF, RB, 256), F32),
                pltpu.VMEM((2, 64, 2 * T), F32),
                pltpu.VMEM((2, 64, 2 * T), BF16),
                dma(()), dma((NW,)), dma((NW,)), dma((NC,)), dma((NC,)), dma((2,)),
                dma(()), dma(()),
                dma(()), dma((NC,)),
                dma(()), dma((NC,)),
                dma(()), dma((NC,)),
                dma(()), dma((NC,)),
                dma(()), dma((NC,)),
                dma(()), dma(()),
                dma(()), dma((NC,)),
                dma(()), dma((NC,)),
                dma(()), dma((NC,)),
                dma(()), dma((NC,)),
            ],
            compiler_params=pltpu.CompilerParams(
                collective_id=0, has_side_effects=True, vmem_limit_bytes=52 * 1024 * 1024),
            name="decode",
        )(seq_lens, x_hidden, k2, v2, wq2, wo2)

    return jax.shard_map(
        local_step,
        mesh=mesh,
        in_specs=(P('dp', None), P('dp'), P('dp', 'seq', 'kvh', None), P('dp', 'seq', 'kvh', None),
                  P(None, ('kvh', 'seq'), None), P(('kvh', 'seq'), None, None)),
        out_specs=P('dp', None),
        check_vma=False)
```

time: 61.6 us -> 46.5 us (0.75)
  Pallas kernels: 58.6 us -> 44.7 us
  local copies, waits for them, and re-layouts: 2.29 us -> 1.63 us
    pallas_call x1, Pallas kernels: 58.6 us -> 44.7 us  [local_step(): pl.pallas_call(kernel, out_shape=jax.ShapeDtypeStruct((ROWS, D), BF16), i...]
    unnamed x1 -> x3, local copies, waits for them, and re-layouts: 2.29 us -> 1.63 us
where the time goes in v2:
time: 46.5 us; the launch traced here: 46.3 us
  Pallas kernels  44.7 us (96%)
  local copies, waits for them, and re-layouts  1.63 us (4%)
    pallas_call x1, Pallas kernels, local_step(): pl.pallas_call(kernel, out_shape=jax.ShapeDtypeStruct((ROWS, D), BF16), i...  44.7 us
    unnamed x3, local copies, waits for them, and re-layouts  1.63 us

profile of v2, /device:TPU:0, one launch (start us, length us, event | category | flops | bytes accessed | tf_op | source)
XLA Modules:
  0.0 46.3 jit_solution(15239913303320688206)
XLA Ops:
  0.0 0.0 copy-start
  0.0 0.7 %copy-done = s32[128]{0:T(128)S(1)} copy-done((s32[128]{0:T(128)S(1)}, s32[128]{0:T(128)}, u32[]{:S(2)}) %copy-start) | copy-done | bytes 536
  0.7 44.7 %decode.1 = bf16[128,4096]{1,0:T(8,128)(2,1)S(1)} custom-call(s32[128]{0:T(128)S(1)} %copy-done, bf16[128,4096]{1,0:T(8,128)(2,1)} %x_h.1, bf16[128,512,128]{2,1,0:T(8,128)(2,1)} %bitcast.4, bf16[128,512,128]{2,1,0:T(8,128)(2,1)} %bitcast.5, bf16[8192,128]{1,0:T(8,128)(2,1)} %bitcast.6, bf16[256,4096]{1,0:T(8,128)(2,1)} %bitcast.7), custom_call_target="tpu_custom_call" | custom-call | tf_op jit(solution)/shard_map/decode/pallas_call | solution.py:449
  45.4 1.0 %copy.8 = bf16[128,4096]{1,0:T(8,128)(2,1)} copy(bf16[128,4096]{1,0:T(8,128)(2,1)S(1)} %decode.1) | data formatting | bytes 2097152
Async XLA Ops:
  0.0 0.7 %copy-start = (s32[128]{0:T(128)S(1)}, s32[128]{0:T(128)}, u32[]{:S(2)}) copy-start(s32[128]{0:T(128)} %lens_h.1) | copy-start | bytes 1540

commit v3 on v2

--- a/solution.py
+++ b/solution.py
@@ -29,43 +29,13 @@
 Z_FIRST = (0, 1, 2)
 NF = len(Z_FIRST)
 
-WORK = (0.97, 0.17, 0.42, 0.1, 0.08, 0.03, 0.02, 0.01)
-LAT = (2.4, 1.1, 2.4, 3.6, 3.4, 2.4, 1.1)
-WIRE = (0.86, 0.1, 1.4, 1.4, 0.7, 0.7, 0.1)
-LINK = (0, 1, 0, 2, 2, 0, 1)
-Z_PATH = {2: (3.6, 2.8, 2), 3: (2.4, 0.35, 0)}
-PRIO = (7, 6, 5, 4, 3, 2, 1, 0)
-Q_AT, Q_STEP, KV_AT, KV_STEP = 6.0, 0.35, 3.5, 1.27
-
-
-def event_order():
-    ready = {(0, 0): max(Q_AT, KV_AT + KV_STEP)}
-    link_free = [0.0, 0.0, 0.0]
-    now, order, last = 0.0, [], len(WORK) - 1
-    while ready:
-        can = [e for e, t in ready.items() if t <= now]
-        if not can:
-            now = min(ready.values())
-            continue
-        stage, c = min(can, key=lambda e: (PRIO[e[0]], e[1]))
-        del ready[stage, c]
-        order.append((stage, c))
-        now += WORK[stage] * (0.55 if stage == 0 and c in (0, NC) else 1.0)
-        if stage == 0:
-            if c < NC:
-                n = min(c + 1, NC - 1)
-                ready[0, c + 1] = max(Q_AT + Q_STEP * n, KV_AT + KV_STEP * (n + 1))
-            if c == 0:
-                continue
-            c -= 1
-        if stage < last:
-            lat, wire, link = LAT[stage], WIRE[stage], LINK[stage]
-            if c in Z_FIRST and stage in Z_PATH:
-                lat, wire, link = Z_PATH[stage]
-            start = max(now, link_free[link])
-            link_free[link] = start + wire
-            ready[stage + 1, c] = start + wire + lat
-    return order
+ORDER = (
+    (0, 0), (0, 1), (0, 2), (0, 3), (0, 4), (1, 0), (0, 5), (1, 1), (2, 0), (2, 1), (0, 6), (1, 3), (0, 7),
+    (2, 3), (1, 4), (1, 2), (0, 8), (2, 2), (2, 4), (1, 5), (3, 0), (1, 6), (2, 5), (2, 6), (3, 3), (3, 1),
+    (1, 7), (3, 4), (2, 7), (4, 0), (3, 5), (4, 3), (3, 2), (3, 6), (3, 7), (5, 0), (4, 1), (4, 5), (4, 2),
+    (5, 3), (4, 4), (4, 6), (4, 7), (5, 1), (5, 2), (5, 5), (5, 4), (5, 6), (5, 7), (6, 2), (6, 0), (6, 1),
+    (6, 5), (6, 4), (7, 1), (6, 6), (7, 0), (6, 7), (6, 3), (7, 2), (7, 4), (7, 6), (7, 7), (7, 5), (7, 3),
+)
 
 
 def kernel(lens_h, x_h, k_h, v_h, wq_h, wo_h, out_v,
@@ -150,7 +120,6 @@
                 wo_cp(i).start()
         return carry
 
-    lax.fori_loop(0, NC, load_body, 0)
     lens_cp.wait()
 
     sub8 = lax.broadcasted_iota(jnp.int32, (8, 128), 0)
@@ -176,6 +145,8 @@
     for i in range(NW):
         x_cp(i).wait()
         wq_cp(i).wait()
+        if i == 2:
+            lax.fori_loop(0, NC, load_body, 0)
         slot = i % 2
         wf_v[slot] = wq_v[pl.ds(i * WR, WR), :].astype(F32)
         w0 = wf_v[slot, pl.ds(0, WR // 2, 2), :].astype(BF16)
@@ -274,17 +245,20 @@
             o_cp(c, d).start()
 
     def attention(k):
-        if k > 0:
-            v_cp(k - 1).wait()
+        done = 0 if k == 0 else k - 1
+        if k != 1:
+            v_cp(done).wait()
         if k < NC:
             r0 = issue_scores(k)
-        if k > 0:
-            softmax(k - 1)
+        if k > 1:
+            softmax(done)
         if k < NC:
             scores(r0)
-        if k > 0:
-            weighted(k - 1)
-            send_o(k - 1)
+        if k == 0:
+            softmax(done)
+        if k != 1:
+            weighted(done)
+            send_o(done)
 
     def a_cp(c):
         rows = pl.ds(pl.multiple_of(c * RB, RB), RB)
@@ -422,7 +396,7 @@
         ed_cp(c, peer_half + (1 - yy) * 1024).wait_recv()
 
     stages = (attention, stage_b, stage_c, stage_d, stage_e, stage_f, stage_g, stage_h)
-    for stage, c in event_order():
+    for stage, c in ORDER:
         stages[stage](c)
 
     sent(q_all.at[pl.ds(0, 3)], q_ss)

time: 46.5 us -> 45.5 us (0.978)
  Pallas kernels: 44.7 us -> 43.8 us
    pallas_call x1, Pallas kernels: 44.7 us -> 43.8 us  [local_step(): pl.pallas_call(kernel, out_shape=jax.ShapeDtypeStruct((ROWS, D), BF16), i...]
where the time goes in v3:
time: 45.5 us; the launch traced here: 45.4 us
  Pallas kernels  43.8 us (96%)
  local copies, waits for them, and re-layouts  1.63 us (4%)
    pallas_call x1, Pallas kernels, local_step(): pl.pallas_call(kernel, out_shape=jax.ShapeDtypeStruct((ROWS, D), BF16), i...  43.8 us
    unnamed x3, local copies, waits for them, and re-layouts  1.63 us

profile of v3, /device:TPU:0, one launch (start us, length us, event | category | flops | bytes accessed | tf_op | source)
XLA Modules:
  0.0 45.4 jit_solution(4105116658915729218)
XLA Ops:
  0.0 0.0 copy-start
  0.0 0.7 %copy-done = s32[128]{0:T(128)S(1)} copy-done((s32[128]{0:T(128)S(1)}, s32[128]{0:T(128)}, u32[]{:S(2)}) %copy-start) | copy-done | bytes 536
  0.7 43.8 %decode.1 = bf16[128,4096]{1,0:T(8,128)(2,1)S(1)} custom-call(s32[128]{0:T(128)S(1)} %copy-done, bf16[128,4096]{1,0:T(8,128)(2,1)} %x_h.1, bf16[128,512,128]{2,1,0:T(8,128)(2,1)} %bitcast.4, bf16[128,512,128]{2,1,0:T(8,128)(2,1)} %bitcast.5, bf16[8192,128]{1,0:T(8,128)(2,1)} %bitcast.6, bf16[256,4096]{1,0:T(8,128)(2,1)} %bitcast.7), custom_call_target="tpu_custom_call" | custom-call | tf_op jit(solution)/shard_map/decode/pallas_call | solution.py:423
  44.4 1.0 %copy.8 = bf16[128,4096]{1,0:T(8,128)(2,1)} copy(bf16[128,4096]{1,0:T(8,128)(2,1)S(1)} %decode.1) | data formatting | bytes 2097152
Async XLA Ops:
  0.0 0.7 %copy-start = (s32[128]{0:T(128)S(1)}, s32[128]{0:T(128)}, u32[]{:S(2)}) copy-start(s32[128]{0:T(128)} %lens_h.1) | copy-start | bytes 1540

commit v4 on v3

--- a/solution.py
+++ b/solution.py
@@ -30,11 +30,11 @@
 NF = len(Z_FIRST)
 
 ORDER = (
-    (0, 0), (0, 1), (0, 2), (0, 3), (0, 4), (1, 0), (0, 5), (1, 1), (2, 0), (2, 1), (0, 6), (1, 3), (0, 7),
-    (2, 3), (1, 4), (1, 2), (0, 8), (2, 2), (2, 4), (1, 5), (3, 0), (1, 6), (2, 5), (2, 6), (3, 3), (3, 1),
-    (1, 7), (3, 4), (2, 7), (4, 0), (3, 5), (4, 3), (3, 2), (3, 6), (3, 7), (5, 0), (4, 1), (4, 5), (4, 2),
-    (5, 3), (4, 4), (4, 6), (4, 7), (5, 1), (5, 2), (5, 5), (5, 4), (5, 6), (5, 7), (6, 2), (6, 0), (6, 1),
-    (6, 5), (6, 4), (7, 1), (6, 6), (7, 0), (6, 7), (6, 3), (7, 2), (7, 4), (7, 6), (7, 7), (7, 5), (7, 3),
+    (0, 0), (0, 1), (0, 2), (0, 3), (0, 4), (1, 0), (0, 5), (1, 1), (2, 0), (0, 6), (0, 7), (1, 3), (2, 1),
+    (0, 8), (1, 4), (1, 2), (2, 3), (2, 2), (1, 6), (2, 4), (1, 5), (1, 7), (3, 3), (3, 0), (2, 5), (2, 6),
+    (3, 1), (2, 7), (3, 4), (4, 0), (3, 5), (4, 1), (3, 2), (3, 6), (3, 7), (4, 2), (4, 3), (4, 5), (5, 1),
+    (4, 4), (4, 6), (5, 0), (4, 7), (5, 2), (5, 3), (5, 5), (6, 1), (5, 4), (5, 6), (5, 7), (6, 5), (6, 2),
+    (6, 4), (6, 6), (7, 2), (6, 3), (7, 1), (6, 0), (6, 7), (7, 5), (7, 4), (7, 3), (7, 0), (7, 6), (7, 7),
 )
 
 
@@ -145,7 +145,7 @@
     for i in range(NW):
         x_cp(i).wait()
         wq_cp(i).wait()
-        if i == 2:
+        if i == 1:
             lax.fori_loop(0, NC, load_body, 0)
         slot = i % 2
         wf_v[slot] = wq_v[pl.ds(i * WR, WR), :].astype(F32)

time: 45.5 us -> 45.1 us (level)
  Pallas kernels: 43.8 us -> 43.3 us
where the time goes in v4:
time: 45.1 us; the launch traced here: 45 us
  Pallas kernels  43.3 us (96%)
  local copies, waits for them, and re-layouts  1.63 us (4%)
    pallas_call x1, Pallas kernels, local_step(): pl.pallas_call(kernel, out_shape=jax.ShapeDtypeStruct((ROWS, D), BF16), i...  43.3 us
    unnamed x3, local copies, waits for them, and re-layouts  1.63 us

profile of v4, /device:TPU:0, one launch (start us, length us, event | category | flops | bytes accessed | tf_op | source)
XLA Modules:
  0.0 45.0 jit_solution(13166443097182374300)
XLA Ops:
  0.0 0.0 copy-start
  0.0 0.7 %copy-done = s32[128]{0:T(128)S(1)} copy-done((s32[128]{0:T(128)S(1)}, s32[128]{0:T(128)}, u32[]{:S(2)}) %copy-start) | copy-done | bytes 536
  0.7 43.3 %decode.1 = bf16[128,4096]{1,0:T(8,128)(2,1)S(1)} custom-call(s32[128]{0:T(128)S(1)} %copy-done, bf16[128,4096]{1,0:T(8,128)(2,1)} %x_h.1, bf16[128,512,128]{2,1,0:T(8,128)(2,1)} %bitcast.4, bf16[128,512,128]{2,1,0:T(8,128)(2,1)} %bitcast.5, bf16[8192,128]{1,0:T(8,128)(2,1)} %bitcast.6, bf16[256,4096]{1,0:T(8,128)(2,1)} %bitcast.7), custom_call_target="tpu_custom_call" | custom-call | tf_op jit(solution)/shard_map/decode/pallas_call | solution.py:423
  44.0 1.0 %copy.8 = bf16[128,4096]{1,0:T(8,128)(2,1)} copy(bf16[128,4096]{1,0:T(8,128)(2,1)S(1)} %decode.1) | data formatting | bytes 2097152
Async XLA Ops:
  0.0 0.7 %copy-start = (s32[128]{0:T(128)S(1)}, s32[128]{0:T(128)}, u32[]{:S(2)}) copy-start(s32[128]{0:T(128)} %lens_h.1) | copy-start | bytes 1540

commit v5 on v4

--- a/solution.py
+++ b/solution.py
@@ -30,11 +30,11 @@
 NF = len(Z_FIRST)
 
 ORDER = (
-    (0, 0), (0, 1), (0, 2), (0, 3), (0, 4), (1, 0), (0, 5), (1, 1), (2, 0), (0, 6), (0, 7), (1, 3), (2, 1),
-    (0, 8), (1, 4), (1, 2), (2, 3), (2, 2), (1, 6), (2, 4), (1, 5), (1, 7), (3, 3), (3, 0), (2, 5), (2, 6),
-    (3, 1), (2, 7), (3, 4), (4, 0), (3, 5), (4, 1), (3, 2), (3, 6), (3, 7), (4, 2), (4, 3), (4, 5), (5, 1),
-    (4, 4), (4, 6), (5, 0), (4, 7), (5, 2), (5, 3), (5, 5), (6, 1), (5, 4), (5, 6), (5, 7), (6, 5), (6, 2),
-    (6, 4), (6, 6), (7, 2), (6, 3), (7, 1), (6, 0), (6, 7), (7, 5), (7, 4), (7, 3), (7, 0), (7, 6), (7, 7),
+    (0, 0), (0, 1), (0, 2), (0, 3), (1, 0), (0, 4), (2, 0), (1, 1), (0, 5), (0, 6), (2, 1), (1, 3), (0, 7),
+    (1, 4), (2, 3), (1, 2), (0, 8), (2, 2), (2, 4), (1, 5), (1, 6), (2, 5), (3, 0), (3, 3), (3, 1), (2, 6),
+    (1, 7), (3, 4), (2, 7), (3, 5), (4, 0), (4, 3), (3, 6), (4, 1), (3, 7), (3, 2), (4, 2), (4, 4), (5, 3),
+    (4, 5), (4, 6), (5, 0), (5, 1), (4, 7), (6, 0), (5, 4), (6, 3), (5, 2), (6, 1), (5, 5), (5, 6), (5, 7),
+    (6, 5), (6, 4), (6, 6), (6, 2), (6, 7), (7, 2), (7, 0), (7, 5), (7, 6), (7, 1), (7, 3), (7, 4), (7, 7),
 )
 
 

time: 45.1 us -> 45.4 us (level)
  no operation moved by 1% of the time
where the time goes in v5:
time: 45.4 us; the launch traced here: 45.3 us
  Pallas kernels  43.6 us (96%)
  local copies, waits for them, and re-layouts  1.63 us (4%)
    pallas_call x1, Pallas kernels, local_step(): pl.pallas_call(kernel, out_shape=jax.ShapeDtypeStruct((ROWS, D), BF16), i...  43.6 us
    unnamed x3, local copies, waits for them, and re-layouts  1.63 us

profile of v5, /device:TPU:0, one launch (start us, length us, event | category | flops | bytes accessed | tf_op | source)
XLA Modules:
  0.0 45.3 jit_solution(17043782410097237772)
XLA Ops:
  0.0 0.0 copy-start
  0.0 0.7 %copy-done = s32[128]{0:T(128)S(1)} copy-done((s32[128]{0:T(128)S(1)}, s32[128]{0:T(128)}, u32[]{:S(2)}) %copy-start) | copy-done | bytes 536
  0.7 43.6 %decode.1 = bf16[128,4096]{1,0:T(8,128)(2,1)S(1)} custom-call(s32[128]{0:T(128)S(1)} %copy-done, bf16[128,4096]{1,0:T(8,128)(2,1)} %x_h.1, bf16[128,512,128]{2,1,0:T(8,128)(2,1)} %bitcast.4, bf16[128,512,128]{2,1,0:T(8,128)(2,1)} %bitcast.5, bf16[8192,128]{1,0:T(8,128)(2,1)} %bitcast.6, bf16[256,4096]{1,0:T(8,128)(2,1)} %bitcast.7), custom_call_target="tpu_custom_call" | custom-call | tf_op jit(solution)/shard_map/decode/pallas_call | solution.py:423
  44.3 1.0 %copy.8 = bf16[128,4096]{1,0:T(8,128)(2,1)} copy(bf16[128,4096]{1,0:T(8,128)(2,1)S(1)} %decode.1) | data formatting | bytes 2097152
Async XLA Ops:
  0.0 0.7 %copy-start = (s32[128]{0:T(128)S(1)}, s32[128]{0:T(128)}, u32[]{:S(2)}) copy-start(s32[128]{0:T(128)} %lens_h.1) | copy-start | bytes 1540
